TPU v7x, 32 devices: a whole 2x2x4 slice. The times are simulated.
32 devices in a mesh: tile: 8 (over y, x, core), head: 4 (over z).
Axes of the slice: x: 2, y: 2, z: 4, core: 2. Of those that a mesh axis runs over, the one named last changes fastest.
Arguments:
- latent: bfloat16 [16, 512, 512], P('tile', 'head'), may hold values from -6 to 6
- norm1_gain: float32 [512], replicated, may hold values from 0.25 to 1.75
- norm1_shift: float32 [512], replicated, may hold values from -1.75 to 1.75
- conv1_weight: bfloat16 [3, 3, 512, 512], replicated, may hold values from -0.09375 to 0.09375
- conv1_bias: float32 [512], replicated, may hold values from -1.75 to 1.75
- norm2_gain: float32 [512], replicated, may hold values from 0.25 to 1.75
- norm2_shift: float32 [512], replicated, may hold values from -1.75 to 1.75
- conv2_weight: bfloat16 [3, 3, 512, 512], replicated, may hold values from -0.09375 to 0.09375
- conv2_bias: float32 [512], replicated, may hold values from -1.75 to 1.75
- norm3_gain: float32 [512], replicated, may hold values from 0.25 to 1.75
- norm3_shift: float32 [512], replicated, may hold values from -1.75 to 1.75
- query_weight: bfloat16 [512, 512], replicated, may hold values from -2 to 2
- query_bias: float32 [512], replicated, may hold values from -3 to 3
- key_weight: bfloat16 [512, 512], replicated, may hold values from -2 to 2
- value_weight: bfloat16 [512, 512], replicated, may hold values from -0.25 to 0.25
- value_bias: float32 [512], replicated, may hold values from -3 to 3
- out_weight: bfloat16 [512, 512], replicated, may hold values from -0.5 to 0.5
- out_bias: float32 [512], replicated, may hold values from -1.75 to 1.75
Outputs:
- block_out: bfloat16 [16, 512, 512], P('tile', 'head')
All inputs are finite; a program needn't handle non-finite values.
Results may differ from a plain program's by a relative error of at most 0.01615.
Values may be sent and summed in bfloat16 or wider, within the bound.
A program may use at most 128 MiB of HBM per device.

v0:
```python
import jax
import jax.numpy as jnp
from jax import lax
from jax.sharding import PartitionSpec as P

C = 512
GROUPS = 32


def extended(x, sides, width):
    for axis, dim in sides:
        peers, length = (lax.axis_size(axis), x.shape[dim])
        up = [(i, (i + 1) % peers) for i in range(peers - 1)]
        down = [(j, i) for i, j in up]
        last = lax.slice_in_dim(x, length - width, length, axis=dim)
        initial = lax.slice_in_dim(x, 0, width, axis=dim)
        before = lax.ppermute(last, axis, up)
        after = lax.ppermute(initial, axis, down)
        x = jnp.concatenate([before, x, after], axis=dim)
    return x


def group_norm(values, gain, shift, members):
    grouped = values.reshape(-1, GROUPS, C // GROUPS)
    sums = lax.psum(jnp.sum(grouped, axis=(0, 2)), ("tile", "head"))
    mean = sums / members
    deviation = grouped - mean[None, :, None]
    variance = lax.psum(jnp.sum(deviation * deviation, axis=(0, 2)), ("tile", "head")) / members
    normalized = deviation * lax.rsqrt(variance + 1e-06)[None, :, None]
    return normalized.reshape(values.shape) * gain + shift


def conv_three(act, weight, bias):
    padded = extended(act, (("tile", 0), ("head", 1)), 1)
    result = lax.conv_general_dilated(
        padded[None],
        weight,
        (1, 1),
        "VALID",
        dimension_numbers=("NHWC", "HWIO", "NHWC"),
        preferred_element_type=jnp.float32,
    )[0]
    return result + bias


def per_device(
    latent,
    norm1_gain,
    norm1_shift,
    conv1_weight,
    conv1_bias,
    norm2_gain,
    norm2_shift,
    conv2_weight,
    conv2_bias,
    norm3_gain,
    norm3_shift,
    query_weight,
    query_bias,
    key_weight,
    value_weight,
    value_bias,
    out_weight,
    out_bias,
):
    local_rows, local_cols, channels = latent.shape
    positions = local_rows * local_cols
    members = positions * lax.axis_size("tile") * lax.axis_size("head") * (C // GROUPS)
    latent32 = latent.astype(jnp.float32).reshape(positions, C)
    act1 = jax.nn.silu(group_norm(latent32, norm1_gain, norm1_shift, members)).astype(jnp.bfloat16)
    hidden = conv_three(act1.reshape(local_rows, local_cols, C), conv1_weight, conv1_bias).reshape(
        positions, C
    )
    act2 = jax.nn.silu(group_norm(hidden, norm2_gain, norm2_shift, members)).astype(jnp.bfloat16)
    second = conv_three(act2.reshape(local_rows, local_cols, C), conv2_weight, conv2_bias).reshape(
        positions, C
    )
    resid = (latent32 + second).astype(jnp.bfloat16)
    normed = group_norm(resid.astype(jnp.float32), norm3_gain, norm3_shift, members).astype(
        jnp.bfloat16
    )
    queries = (
        jnp.dot(normed, query_weight, preferred_element_type=jnp.float32) + query_bias
    ).astype(jnp.bfloat16)
    tile_queries = lax.all_gather(queries, "head", axis=0, tiled=True)
    query_rows = tile_queries.shape[0]
    softmax_scale = 1.0 / C**0.5
    widest = positions * max(1, 2048 // positions)
    initial = (
        jnp.full((query_rows,), -1e30, jnp.float32),
        jnp.zeros((query_rows,), jnp.float32),
        jnp.zeros((query_rows, C), jnp.float32),
    )
    keys = jnp.dot(normed, key_weight, preferred_element_type=jnp.float32).astype(jnp.bfloat16)
    values = (
        jnp.dot(normed, value_weight, preferred_element_type=jnp.float32) + value_bias
    ).astype(jnp.bfloat16)
    key_rows = lax.all_gather(keys, "tile", axis=0, tiled=True)
    rows_here = key_rows.shape[0]
    block_len = min(rows_here, widest)
    while rows_here % block_len != 0:
        block_len = block_len - positions
    nblocks = rows_here // block_len

    def step_block(state_in, block_pair):
        run_max, run_sum, weighted = state_in
        key_block, value_block = block_pair
        scores = (
            jnp.dot(tile_queries, key_block.T, preferred_element_type=jnp.float32) * softmax_scale
        )
        new_max = jnp.maximum(run_max, jnp.max(scores, axis=1))
        factor = jnp.exp(run_max - new_max)
        expo = jnp.exp(scores - new_max[:, None])
        run_sum = run_sum * factor + jnp.sum(expo, axis=1)
        weighted = weighted * factor[:, None] + jnp.dot(
            expo.astype(jnp.bfloat16), value_block, preferred_element_type=jnp.float32
        )
        return ((new_max, run_sum, weighted), None)

    blocked = (
        key_rows.reshape(nblocks, block_len, C),
        lax.all_gather(values, "tile", axis=0, tiled=True).reshape(nblocks, block_len, C),
    )
    state_out, unused = lax.scan(step_block, initial, blocked)
    run_max, run_sum, weighted = state_out
    top = lax.pmax(run_max, "head")
    factor = jnp.exp(run_max - top)
    own_weighted, own_sum = (
        lax.psum_scatter(
            (weighted * factor[:, None]).astype(jnp.bfloat16),
            "head",
            scatter_dimension=0,
            tiled=True,
        ).astype(jnp.float32),
        lax.psum_scatter(
            (run_sum * factor).astype(jnp.bfloat16), "head", scatter_dimension=0, tiled=True
        ).astype(jnp.float32),
    )
    attended = (own_weighted / own_sum[:, None]).astype(jnp.bfloat16)
    mixed = (
        resid.astype(jnp.float32)
        + jnp.dot(attended, out_weight, preferred_element_type=jnp.float32)
        + out_bias
    )
    return mixed.astype(jnp.bfloat16).reshape(local_rows, local_cols, C)


def solution(mesh):
    return jax.shard_map(
        per_device,
        mesh=mesh,
        in_specs=(
            P("tile", "head", None),
            P(),
            P(),
            P(),
            P(),
            P(),
            P(),
            P(),
            P(),
            P(),
            P(),
            P(),
            P(),
            P(),
            P(),
            P(),
            P(),
            P(),
        ),
        out_specs=P("tile", "head", None),
        check_vma=False,
    )
```

profile of v0, /device:TPU:0, one launch (start us, length us, event | category | flops | bytes accessed | tf_op | source)
XLA Modules:
  0.0 429.3 jit_solution(8962881131567020059)
XLA Ops:
  6.5 1.1 convert_reduce_fusion.1
  7.8 42.0 %psum.42 = f32[32]{0:T(128)S(1)} all-reduce(f32[32]{0:T(128)S(1)} %reduce_sum.83), channel_id=1, replica_groups=mesh['tile'=8,'head'=4] {'tile','head'}, use_global_device_ids=true, to_apply=%region_2.0 | all-reduce | flops 32 | bytes 256 | tf_op jit(solution)/shard_map/psum | solution.py:25
  50.0 1.0 fusion.46
  51.2 40.1 %psum.43 = f32[32]{0:T(128)S(1)} all-reduce(f32[32]{0:T(128)S(1)} %reduce_sum.89), channel_id=1, replica_groups=mesh['tile'=8,'head'=4] {'tile','head'}, use_global_device_ids=true, to_apply=%region_5.6 | all-reduce | flops 32 | bytes 256 | tf_op jit(solution)/shard_map/psum | solution.py:28
  91.5 1.2 fusion.63
  92.7 1.3 collective-permute-start
  94.0 1.3 collective-permute-start.1
  95.3 1.2 fusion.54
  96.5 3.3 collective-permute-done.1
  99.8 2.6 collective-permute-start.2
  102.4 1.3 collective-permute-start.3
  103.8 4.2 collective-permute-done.3
  108.1 0.3 copy.59
  108.4 0.2 pad.clone
  108.8 1.5 select_reduce_fusion.1
  110.5 42.0 %psum.44 = f32[32]{0:T(128)S(1)} all-reduce(f32[32]{0:T(128)S(1)} %reduce_sum.92), channel_id=1, replica_groups=mesh['tile'=8,'head'=4] {'tile','head'}, use_global_device_ids=true, to_apply=%region_8.9 | all-reduce | flops 32 | bytes 256 | tf_op jit(solution)/shard_map/psum | solution.py:25
  152.7 0.2 select_reduce_fusion
  153.0 0.4 copy.50
  153.5 39.9 %psum.45 = f32[32]{0:T(128)S(1)} all-reduce(f32[32]{0:T(128)S(1)} %reduce_sum.117), channel_id=1, replica_groups=mesh['tile'=8,'head'=4] {'tile','head'}, use_global_device_ids=true, to_apply=%region_11.12 | all-reduce | flops 32 | bytes 256 | tf_op jit(solution)/shard_map/psum | solution.py:28
  193.7 0.2 multiply_convert_fusion.2
  194.0 1.3 collective-permute-start.4
  195.3 1.3 collective-permute-start.5
  196.6 0.2 multiply_convert_fusion.1
  196.8 4.2 collective-permute-done.5
  201.0 3.4 collective-permute-start.6
  204.4 1.3 collective-permute-start.7
  205.8 4.2 collective-permute-done.7
  210.1 0.3 copy.60
  210.4 0.2 pad.2.clone
  210.8 3.8 convolution_select_fusion
  214.6 0.4 copy.55
  215.1 0.4 copy-done.1
  215.9 41.5 %psum.46 = f32[32]{0:T(128)S(1)} all-reduce(f32[32]{0:T(128)S(1)} %reduce_sum.120), channel_id=1, replica_groups=mesh['tile'=8,'head'=4] {'tile','head'}, use_global_device_ids=true, to_apply=%region_14.15 | all-reduce | flops 32 | bytes 256 | tf_op jit(solution)/shard_map/psum | solution.py:25
  258.0 40.5 %psum.47 = f32[32]{0:T(128)S(1)} all-reduce(f32[32]{0:T(128)S(1)} %reduce_sum.123), channel_id=1, replica_groups=mesh['tile'=8,'head'=4] {'tile','head'}, use_global_device_ids=true, to_apply=%region_17.18 | all-reduce | flops 32 | bytes 256 | tf_op jit(solution)/shard_map/psum | solution.py:28
  298.8 1.0 fusion.12
  299.9 1.0 convolution_convert_fusion
  301.0 1.0 fusion.13
  302.1 24.9 %all-gather.4.cloned.1.call-done = bf16[1024,512]{1,0:T(8,128)(2,1)} async-done(((bf16[256,512]{1,0:T(8,128)(2,1)}), bf16[1024,512]{1,0:T(8,128)(2,1)}) %all-gather.4.cloned.1.call-update) | async-done | bytes 1048592 | tf_op jit(solution)/shard_map/all_gather | solution.py:85
  327.0 29.1 %all-gather.6.cloned.1.call-done = bf16[2048,512]{1,0:T(8,128)(2,1)} async-done(((bf16[256,512]{1,0:T(8,128)(2,1)}), bf16[2048,512]{1,0:T(8,128)(2,1)}) %all-gather.6.cloned.1.call-update) | async-done | bytes 2097168 | tf_op jit(solution)/shard_map/all_gather | solution.py:98
  356.1 7.5 %multiply_reduce_fusion = (f32[1024]{0:T(1024)S(1)}, f32[1024,2048]{1,0:T(8,128)}) fusion(bf16[1024,512]{1,0:T(8,128)(2,1)} %all-gather.4.cloned.1.call-done, bf16[2048,512]{1,0:T(8,128)(2,1)} %all-gather.6.cloned.1.call-done), kind=kOutput, calls=%fused_computation.1 | convolution fusion | flops 2151676928 | bytes 11538432 | tf_op jit(solution)/shard_map/while/body/eval_jaxpr/dot_general | solution.py:109
  363.6 11.7 %pmax.7 = f32[1024]{0:T(1024)S(1)} all-reduce(f32[1024]{0:T(1024)S(1)} %broadcast_maximum_fusion), channel_id=1, replica_groups=mesh['tile'=8,'head'=4] {'head'}, use_global_device_ids=true, to_apply=%region_19.20 | all-reduce | flops 1024 | bytes 8192 | tf_op jit(solution)/shard_map/pmax | solution.py:126
  375.2 4.7 %fusion = f32[1024]{0:T(1024)S(1)} fusion(f32[1024,2048]{1,0:T(8,128)} %get-tuple-element.42, f32[1024]{0:T(1024)S(1)} %broadcast_maximum_fusion), kind=kLoop, calls=%fused_computation.2 | loop fusion | flops 6290432 | bytes 8396800 | tf_op jit(solution)/shard_map/while/body/eval_jaxpr/reduce_sum | solution.py:114
  380.0 5.8 %all-gather.8.cloned.1.call-done = bf16[2048,512]{1,0:T(8,128)(2,1)} async-done(((bf16[256,512]{1,0:T(8,128)(2,1)}), bf16[2048,512]{1,0:T(8,128)(2,1)}) %all-gather.8.cloned.1.call-update) | async-done | bytes 2097168 | tf_op jit(solution)/shard_map/all_gather | solution.py:122
  385.8 7.4 %multiply_convert_fusion = bf16[1024,512]{1,0:T(8,128)(2,1)} fusion(bf16[2048,512]{1,0:T(8,128)(2,1)} %all-gather.8.cloned.1.call-done, f32[1024,2048]{1,0:T(8,128)} %get-tuple-element.42, f32[1024]{0:T(1024)S(1)} %broadcast_maximum_fusion, f32[1024]{0:T(1024)S(1)} %get-tuple-element.18, f32[1024]{0:T(1024)S(1)} %get-tuple-element.38), kind=kOutput, calls=%fused_computation.7 | convolution fusion | flops 2155347968 | bytes 11546624 | tf_op jit(solution)/shard_map/while/body/eval_jaxpr/dot_general | solution.py:115
  393.2 0.6 dynamic-slice.2
  394.5 12.1 %all-reduce = bf16[1024]{0:T(1024)(128)(2,1)S(1)} all-reduce(bf16[1024]{0:T(1024)(128)(2,1)S(1)} %get-tuple-element.17), channel_id=3, replica_groups=mesh['tile'=8,'head'=4] {'head'}, use_global_device_ids=true, to_apply=%region_22.23.clone | all-reduce | flops 1024 | bytes 4096
  406.6 14.1 %reduce-scatter.2.cloned.1.call-done = bf16[256,512]{1,0:T(8,128)(2,1)} async-done(((bf16[1024,512]{1,0:T(8,128)(2,1)}), bf16[256,512]{1,0:T(8,128)(2,1)}) %reduce-scatter.2.cloned.1.call-update) | async-done | bytes 262160 | tf_op jit(solution)/shard_map/reduce_scatter | solution.py:129
  420.7 2.0 fusion.11
  (95 shorter events, 3.8 us)
Async XLA Ops:
  6.5 292.2 %copy-start = (bf16[512,512]{1,0:T(8,128)(2,1)S(1)}, bf16[512,512]{1,0:T(8,128)(2,1)}, u32[]{:S(2)}) copy-start(bf16[512,512]{1,0:T(8,128)(2,1)} %param.29) | copy-start | bytes 1572868
  6.5 320.4 %all-gather.4.cloned.1.call-start = ((), (), s32[]{:S(2)}) async-start(), calls=%async_computation.1 | async-start | bytes 1310720 | tf_op jit(solution)/shard_map/all_gather | solution.py:85
  92.7 3.8 collective-permute-start
  94.0 5.7 %collective-permute-start.1 = (bf16[1,128,512]{2,1,0:T(8,128)(2,1)S(1)}, bf16[1,128,512]{2,1,0:T(8,128)(2,1)S(1)}, u32[]{:S(2)}, u32[]{:S(2)}) collective-permute-start(bf16[1,128,512]{2,1,0:T(8,128)(2,1)S(1)} %get-tuple-element.37), channel_id=1, source_target_pairs={{4,0},{8,4},{12,8},{16,12},{20,16},{24,20},{28,24},{5,1},{9,5},{13... | collective-permute-start | bytes 393224 | tf_op jit(solution)/shard_map/ppermute | solution.py:18
  99.7 9.0 %copy-start.7 = (bf16[3,3,512,512]{3,2,1,0:T(8,128)(2,1)S(1)}, bf16[3,3,512,512]{3,2,1,0:T(8,128)(2,1)}, u32[]{:S(2)}) copy-start(bf16[3,3,512,512]{3,2,1,0:T(8,128)(2,1)} %param.21) | copy-start | bytes 14155780
  99.8 4.0 collective-permute-start.2
  102.4 6.4 %copy-start.2 = (f32[512]{0:T(512)S(1)}, f32[512]{0:T(512)}, u32[]{:S(2)}) copy-start(f32[512]{0:T(512)} %param.22) | copy-start | bytes 6148
  102.4 6.4 %copy-start.6 = (pred[8,17]{0,1:T(8,128)(4,1)S(1)}, pred[8,17]{0,1:T(8,128)(4,1)}, u32[]{:S(2)}) copy-start(pred[8,17]{0,1:T(8,128)(4,1)} %constant.47) | copy-start | bytes 412
  102.4 5.5 %collective-permute-start.3 = (bf16[4,1,512]{2,1,0:T(2,128)(2,1)S(1)}, bf16[4,1,512]{2,1,0:T(2,128)(2,1)S(1)}, u32[]{:S(2)}, u32[]{:S(2)}) collective-permute-start(bf16[4,1,512]{2,1,0:T(2,128)(2,1)S(1)} %get-tuple-element.33), channel_id=1, source_target_pairs={{1,0},{2,1},{3,2},{5,4},{6,5},{7,6},{9,8},{10,9},{11,10},{13,12},{... | collective-permute-start | bytes 12296 | tf_op jit(solution)/shard_map/ppermute | solution.py:18
  110.3 83.4 %copy-start.3 = (f32[512]{0:T(512)S(1)}, f32[512]{0:T(512)}, u32[]{:S(2)}) copy-start(f32[512]{0:T(512)} %param.24) | copy-start | bytes 6148
  110.3 83.4 %copy-start.4 = (f32[512]{0:T(512)S(1)}, f32[512]{0:T(512)}, u32[]{:S(2)}) copy-start(f32[512]{0:T(512)} %param.23) | copy-start | bytes 6148
  194.0 2.8 collective-permute-start.4
  195.3 5.7 %collective-permute-start.5 = (bf16[1,128,512]{2,1,0:T(8,128)(2,1)S(1)}, bf16[1,128,512]{2,1,0:T(8,128)(2,1)S(1)}, u32[]{:S(2)}, u32[]{:S(2)}) collective-permute-start(bf16[1,128,512]{2,1,0:T(8,128)(2,1)S(1)} %get-tuple-element.35), channel_id=1, source_target_pairs={{4,0},{8,4},{12,8},{16,12},{20,16},{24,20},{28,24},{5,1},{9,5},{13... | collective-permute-start | bytes 393224 | tf_op jit(solution)/shard_map/ppermute | solution.py:18
  201.0 4.8 %collective-permute-start.6 = (bf16[4,1,512]{2,1,0:T(2,128)(2,1)S(1)}, bf16[4,1,512]{2,1,0:T(2,128)(2,1)S(1)}, u32[]{:S(2)}, u32[]{:S(2)}) collective-permute-start(bf16[4,1,512]{2,1,0:T(2,128)(2,1)S(1)} %get-tuple-element.28), channel_id=1, source_target_pairs={{0,1},{1,2},{2,3},{4,5},{5,6},{6,7},{8,9},{9,10},{10,11},{12,13},{... | collective-permute-start | bytes 12296 | tf_op jit(solution)/shard_map/ppermute | solution.py:17
  204.4 5.5 %collective-permute-start.7 = (bf16[4,1,512]{2,1,0:T(2,128)(2,1)S(1)}, bf16[4,1,512]{2,1,0:T(2,128)(2,1)S(1)}, u32[]{:S(2)}, u32[]{:S(2)}) collective-permute-start(bf16[4,1,512]{2,1,0:T(2,128)(2,1)S(1)} %get-tuple-element.30), channel_id=1, source_target_pairs={{1,0},{2,1},{3,2},{5,4},{6,5},{7,6},{9,8},{10,9},{11,10},{13,12},{... | collective-permute-start | bytes 12296 | tf_op jit(solution)/shard_map/ppermute | solution.py:18
  214.6 1.0 copy-start.1
  214.6 0.9 copy-start.5
  215.1 83.7 %copy-start.11 = (f32[512]{0:T(512)S(1)}, f32[512]{0:T(512)}, u32[]{:S(2)}) copy-start(f32[512]{0:T(512)} %param.30) | copy-start | bytes 6148
  215.1 83.7 %copy-start.12 = (f32[512]{0:T(512)S(1)}, f32[512]{0:T(512)}, u32[]{:S(2)}) copy-start(f32[512]{0:T(512)} %param.28) | copy-start | bytes 6148
  215.1 83.7 %copy-start.13 = (f32[512]{0:T(512)S(1)}, f32[512]{0:T(512)}, u32[]{:S(2)}) copy-start(f32[512]{0:T(512)} %param.27) | copy-start | bytes 6148
  257.6 42.3 %copy-start.8 = (bf16[512,512]{1,0:T(8,128)(2,1)S(1)}, bf16[512,512]{1,0:T(8,128)(2,1)}, u32[]{:S(2)}) copy-start(bf16[512,512]{1,0:T(8,128)(2,1)} %param.31) | copy-start | bytes 1572868
  298.6 2.3 copy-start.9
  298.6 2.3 copy-start.14
  299.8 56.2 %all-gather.6.cloned.1.call-start = ((), (), s32[]{:S(2)}) async-start(), calls=%async_computation.2 | async-start | bytes 2359296 | tf_op jit(solution)/shard_map/all_gather | solution.py:98
  300.9 84.8 %all-gather.8.cloned.1.call-start = ((), (), s32[]{:S(2)}) async-start(), calls=%async_computation.3 | async-start | bytes 2359296 | tf_op jit(solution)/shard_map/all_gather | solution.py:122
  302.0 118.7 %reduce-scatter.2.cloned.1.call-start = ((), (), s32[]{:S(2)}) async-start(), calls=%async_computation.4 | async-start | bytes 1310720 | tf_op jit(solution)/shard_map/reduce_scatter | solution.py:129
  385.8 7.4 %copy-start.16 = (u32[32]{0:T(128)S(1)}, u32[32]{0:T(128)}, u32[]{:S(2)}) copy-start(u32[32]{0:T(128)} %constant.53) | copy-start | bytes 388
  385.8 35.0 %copy-start.10 = (bf16[512,512]{1,0:T(8,128)(2,1)S(1)}, bf16[512,512]{1,0:T(8,128)(2,1)}, u32[]{:S(2)}) copy-start(bf16[512,512]{1,0:T(8,128)(2,1)} %param.34) | copy-start | bytes 1572868
  385.8 35.0 %copy-start.15 = (f32[512]{0:T(512)S(1)}, f32[512]{0:T(512)}, u32[]{:S(2)}) copy-start(f32[512]{0:T(512)} %param.35) | copy-start | bytes 6148
Sparse Core Ops, SparseCore 0:
  299.9 26.9 all-gather.3
  328.9 27.1 all-gather.5
  357.9 27.7 all-gather.7
  393.3 27.3 reduce-scatter.1
where the time goes:
time: 430 us; the launch traced here: 429 us
  blocking collectives  270 us (63%)
  waiting for transfers between devices  89.9 us (21%)
  matrix products  25.3 us (6%)
  between operations  14.3 us (3%)
  starting transfers between devices  13.9 us (3%)
  other arithmetic  11.1 us (3%)
  local copies, waits for them, and re-layouts  4.89 us (1%)
    psum x3, blocking collectives, group_norm(): sums = lax.psum(jnp.sum(grouped, axis=(0, 2)), ('tile', 'head'))  126 us
    psum x3, blocking collectives, group_norm(): lax.psum(jnp.sum(deviation * deviation, axis=(0, 2)), ('tile', 'head'))  121 us
    all_gather x1, waiting for transfers between devices, per_device(): key_rows = lax.all_gather(keys, 'tile', axis=0, tiled=True)  29.1 us
    all_gather x1, waiting for transfers between devices, per_device(): tile_queries = lax.all_gather(queries, 'head', axis=0, tiled=True)  24.9 us
    ppermute x4, waiting for transfers between devices, extended(): after = lax.ppermute(initial, axis, down)  15.9 us
    reduce_scatter x1, waiting for transfers between devices, per_device(): lax.psum_scatter((weighted * factor[:, None]).astype(jnp.bfloat16), 'head...  14.1 us
    unnamed x1, blocking collectives  12.1 us
    pmax x1, blocking collectives, per_device(): top = lax.pmax(run_max, 'head')  11.7 us
  transfers between devices with their start and end apart: 12, of which 8 were waited for; matrix products, arithmetic and copies ran while one was open for 4% of the time, Pallas kernels for 0%

commit v1 on v0

--- a/solution.py
+++ b/solution.py
@@ -1,3 +1,4 @@
+import functools
 import jax
 import jax.numpy as jnp
 from jax import lax
@@ -5,6 +6,23 @@
 
 C = 512
 GROUPS = 32
+
+
+def _find_panels(vector, mesh_dim):
+    row_list = [vector]
+    how_many = lax.axis_size(mesh_dim)
+    for it in range(how_many - 1):
+        seen_now = lax.ppermute(
+            row_list[-1], mesh_dim, [(b, (b + 1) % how_many) for b in range(how_many)]
+        )
+        row_list.append(seen_now)
+    aux = jnp.concatenate(row_list[::-1], 0)
+    finding = lax.axis_index(mesh_dim)
+    part_now = jnp.roll(aux, (finding + 1) * vector.shape[0], axis=0)
+    return part_now
+
+
+do_counts = functools.partial(_find_panels, mesh_dim="head")
 
 
 def extended(x, sides, width):
@@ -82,7 +100,7 @@
     queries = (
         jnp.dot(normed, query_weight, preferred_element_type=jnp.float32) + query_bias
     ).astype(jnp.bfloat16)
-    tile_queries = lax.all_gather(queries, "head", axis=0, tiled=True)
+    tile_queries = do_counts(queries)
     query_rows = tile_queries.shape[0]
     softmax_scale = 1.0 / C**0.5
     widest = positions * max(1, 2048 // positions)

time: 430 us -> 401 us (0.933)
  waiting for transfers between devices: 89.9 us -> 57.8 us
  local copies, waits for them, and re-layouts: 4.89 us -> 10.7 us
    all_gather x1, waiting for transfers between devices: 29.1 us -> 0.01 us  [per_device(): key_rows = lax.all_gather(keys, 'tile', axis=0, tiled=True)]
    all_gather x1 -> x0, waiting for transfers between devices: 24.9 us -> none  [per_device(): tile_queries = lax.all_gather(queries, 'head', axis=0, tiled=True)]
    ppermute x0 -> x3, waiting for transfers between devices: none -> 23.9 us  [_find_panels(): lax.ppermute(row_list[-1], mesh_dim, [(b, (b + 1) % how_many) for b in ra...]
    unnamed x39 -> x46, local copies, waits for them, and re-layouts: 1.84 us -> 6.89 us
  transfers between devices with their start and end apart: 12 -> 14, of which waited for: 8 -> 9; matrix products, arithmetic and copies ran while one was open for 4% -> 5% of each run, Pallas kernels for 0% -> 0%
where the time goes in v1:
time: 401 us; the launch traced here: 400 us
  blocking collectives  267 us (67%)
  waiting for transfers between devices  57.8 us (14%)
  matrix products  24.6 us (6%)
  starting transfers between devices  15.4 us (4%)
  between operations  14.3 us (4%)
  other arithmetic  10.8 us (3%)
  local copies, waits for them, and re-layouts  10.7 us (3%)
    psum x3, blocking collectives, group_norm(): sums = lax.psum(jnp.sum(grouped, axis=(0, 2)), ('tile', 'head'))  126 us
    psum x3, blocking collectives, group_norm(): lax.psum(jnp.sum(deviation * deviation, axis=(0, 2)), ('tile', 'head'))  121 us
    ppermute x3, waiting for transfers between devices, _find_panels(): lax.ppermute(row_list[-1], mesh_dim, [(b, (b + 1) % how_many) for b in ra...  23.9 us
    ppermute x4, waiting for transfers between devices, extended(): after = lax.ppermute(initial, axis, down)  15.9 us
    reduce_scatter x1, waiting for transfers between devices, per_device(): lax.psum_scatter((weighted * factor[:, None]).astype(jnp.bfloat16), 'head...  14.1 us
    unnamed x1, blocking collectives  12.1 us
    ppermute x4, starting transfers between devices, extended(): before = lax.ppermute(last, axis, up)  8.65 us
    pmax x1, blocking collectives, per_device(): top = lax.pmax(run_max, 'head')  8.35 us
  transfers between devices with their start and end apart: 14, of which 9 were waited for; matrix products, arithmetic and copies ran while one was open for 5% of the time, Pallas kernels for 0%

profile of v1, /device:TPU:0, one launch (start us, length us, event | category | flops | bytes accessed | tf_op | source)
XLA Modules:
  0.0 400.0 jit_solution(9726510197306035422)
XLA Ops:
  6.5 1.1 convert_reduce_fusion.1
  7.8 42.0 %psum.42 = f32[32]{0:T(128)S(1)} all-reduce(f32[32]{0:T(128)S(1)} %reduce_sum.83), channel_id=1, replica_groups=mesh['tile'=8,'head'=4] {'tile','head'}, use_global_device_ids=true, to_apply=%region_2.0 | all-reduce | flops 32 | bytes 256 | tf_op jit(solution)/shard_map/psum | solution.py:43
  50.0 1.0 fusion.48
  51.2 40.1 %psum.43 = f32[32]{0:T(128)S(1)} all-reduce(f32[32]{0:T(128)S(1)} %reduce_sum.89), channel_id=1, replica_groups=mesh['tile'=8,'head'=4] {'tile','head'}, use_global_device_ids=true, to_apply=%region_5.6 | all-reduce | flops 32 | bytes 256 | tf_op jit(solution)/shard_map/psum | solution.py:46
  91.5 1.2 fusion.65
  92.7 1.3 collective-permute-start
  94.0 1.3 collective-permute-start.1
  95.3 1.2 fusion.56
  96.5 3.3 collective-permute-done.1
  99.8 2.6 collective-permute-start.2
  102.5 1.3 collective-permute-start.3
  103.8 4.2 %collective-permute-done.3 = bf16[4,1,512]{2,1,0:T(2,128)(2,1)S(1)} collective-permute-done((bf16[4,1,512]{2,1,0:T(2,128)(2,1)S(1)}, bf16[4,1,512]{2,1,0:T(2,128)(2,1)S(1)}, u32[]{:S(2)}, u32[]{:S(2)}) %collective-permute-start.3) | collective-permute-done | bytes 4128 | tf_op jit(solution)/shard_map/ppermute | solution.py:36
  108.8 1.5 select_reduce_fusion.1
  110.5 42.0 %psum.44 = f32[32]{0:T(128)S(1)} all-reduce(f32[32]{0:T(128)S(1)} %reduce_sum.92), channel_id=1, replica_groups=mesh['tile'=8,'head'=4] {'tile','head'}, use_global_device_ids=true, to_apply=%region_8.9 | all-reduce | flops 32 | bytes 256 | tf_op jit(solution)/shard_map/psum | solution.py:43
  153.1 0.4 copy.50
  153.5 39.9 %psum.45 = f32[32]{0:T(128)S(1)} all-reduce(f32[32]{0:T(128)S(1)} %reduce_sum.117), channel_id=1, replica_groups=mesh['tile'=8,'head'=4] {'tile','head'}, use_global_device_ids=true, to_apply=%region_11.12 | all-reduce | flops 32 | bytes 256 | tf_op jit(solution)/shard_map/psum | solution.py:46
  194.0 1.3 collective-permute-start.4
  195.3 1.3 collective-permute-start.5
  196.8 4.2 %collective-permute-done.5 = bf16[1,128,512]{2,1,0:T(8,128)(2,1)S(1)} collective-permute-done((bf16[1,128,512]{2,1,0:T(8,128)(2,1)S(1)}, bf16[1,128,512]{2,1,0:T(8,128)(2,1)S(1)}, u32[]{:S(2)}, u32[]{:S(2)}) %collective-permute-start.5) | collective-permute-done | bytes 131104 | tf_op jit(solution)/shard_map/ppermute | solution.py:36
  201.1 3.4 collective-permute-start.6
  204.5 1.3 collective-permute-start.7
  205.8 4.2 %collective-permute-done.7 = bf16[4,1,512]{2,1,0:T(2,128)(2,1)S(1)} collective-permute-done((bf16[4,1,512]{2,1,0:T(2,128)(2,1)S(1)}, bf16[4,1,512]{2,1,0:T(2,128)(2,1)S(1)}, u32[]{:S(2)}, u32[]{:S(2)}) %collective-permute-start.7) | collective-permute-done | bytes 4128 | tf_op jit(solution)/shard_map/ppermute | solution.py:36
  210.8 3.8 convolution_select_fusion
  215.9 41.5 %psum.46 = f32[32]{0:T(128)S(1)} all-reduce(f32[32]{0:T(128)S(1)} %reduce_sum.120), channel_id=1, replica_groups=mesh['tile'=8,'head'=4] {'tile','head'}, use_global_device_ids=true, to_apply=%region_14.15 | all-reduce | flops 32 | bytes 256 | tf_op jit(solution)/shard_map/psum | solution.py:43
  258.0 40.5 %psum.47 = f32[32]{0:T(128)S(1)} all-reduce(f32[32]{0:T(128)S(1)} %reduce_sum.123), channel_id=1, replica_groups=mesh['tile'=8,'head'=4] {'tile','head'}, use_global_device_ids=true, to_apply=%region_17.18 | all-reduce | flops 32 | bytes 256 | tf_op jit(solution)/shard_map/psum | solution.py:46
  298.8 1.0 convolution_convert_fusion
  299.9 1.0 fusion.13
  301.4 1.5 collective-permute-start.8
  302.8 7.6 %collective-permute-done.8 = bf16[256,512]{1,0:T(8,128)(2,1)S(1)} collective-permute-done((bf16[256,512]{1,0:T(8,128)(2,1)S(1)}, bf16[256,512]{1,0:T(8,128)(2,1)S(1)}, u32[]{:S(2)}, u32[]{:S(2)}) %collective-permute-start.8) | collective-permute-done | bytes 262176 | tf_op jit(solution)/shard_map/ppermute | solution.py:15
  310.4 8.2 %collective-permute-done.9 = bf16[256,512]{1,0:T(8,128)(2,1)S(1)} collective-permute-done((bf16[256,512]{1,0:T(8,128)(2,1)S(1)}, bf16[256,512]{1,0:T(8,128)(2,1)S(1)}, u32[]{:S(2)}, u32[]{:S(2)}) %collective-permute-start.9) | collective-permute-done | bytes 262176 | tf_op jit(solution)/shard_map/ppermute | solution.py:15
  318.6 8.2 %collective-permute-done.10 = bf16[256,512]{1,0:T(8,128)(2,1)S(1)} collective-permute-done((bf16[256,512]{1,0:T(8,128)(2,1)S(1)}, bf16[256,512]{1,0:T(8,128)(2,1)S(1)}, u32[]{:S(2)}, u32[]{:S(2)}) %collective-permute-start.10) | collective-permute-done | bytes 262176 | tf_op jit(solution)/shard_map/ppermute | solution.py:15
  326.8 0.7 constant_dynamic-update-slice_fusion.7
  327.5 0.7 constant_dynamic-update-slice_fusion.6
  328.2 0.7 constant_dynamic-update-slice_fusion.5
  329.0 0.7 constant_dynamic-update-slice_fusion.4
  329.7 0.7 constant_dynamic-update-slice_fusion.3
  330.4 0.7 constant_dynamic-update-slice_fusion.2
  331.1 0.7 constant_dynamic-update-slice_fusion.1
  331.8 0.7 constant_dynamic-update-slice_fusion
  332.5 7.5 %multiply_reduce_fusion = (f32[1024]{0:T(1024)S(1)}, f32[1024,2048]{1,0:T(8,128)}) fusion(bf16[2048,512]{1,0:T(8,128)(2,1)} %all-gather.3.cloned.1.call-done, bf16[2048,512]{1,0:T(8,128)(2,1)} %constant_dynamic-update-slice_fusion, s32[]{:T(128)S(6)} %select_n.14), kind=kOutput, calls=%fused_computation.1 | convolution fusion | flops 2151676928 | bytes 11538436 | tf_op jit(solution)/shard_map/while/body/eval_jaxpr/dot_general | solution.py:127
  340.1 8.3 %pmax.7 = f32[1024]{0:T(1024)S(1)} all-reduce(f32[1024]{0:T(1024)S(1)} %broadcast_maximum_fusion), channel_id=1, replica_groups=mesh['tile'=8,'head'=4] {'head'}, use_global_device_ids=true, to_apply=%region_19.20 | all-reduce | flops 1024 | bytes 8192 | tf_op jit(solution)/shard_map/pmax | solution.py:144
  348.4 4.4 %fusion = f32[1024]{0:T(1024)S(1)} fusion(f32[1024,2048]{1,0:T(8,128)} %get-tuple-element.42, f32[1024]{0:T(1024)S(1)} %broadcast_maximum_fusion), kind=kLoop, calls=%fused_computation.2 | loop fusion | flops 6290432 | bytes 8396800 | tf_op jit(solution)/shard_map/while/body/eval_jaxpr/reduce_sum | solution.py:132
  352.8 3.7 all-gather.5.cloned.1.call-done
  356.5 7.4 %multiply_convert_fusion = bf16[1024,512]{1,0:T(8,128)(2,1)} fusion(bf16[2048,512]{1,0:T(8,128)(2,1)} %all-gather.5.cloned.1.call-done, f32[1024,2048]{1,0:T(8,128)} %get-tuple-element.42, f32[1024]{0:T(1024)S(1)} %broadcast_maximum_fusion, f32[1024]{0:T(1024)S(1)} %get-tuple-element.18, f32[1024]{0:T(1024)S(1)} %get-tuple-element.38), kind=kOutput, calls=%fused_computation.7 | convolution fusion | flops 2155347968 | bytes 11546624 | tf_op jit(solution)/shard_map/while/body/eval_jaxpr/dot_general | solution.py:133
  364.0 0.6 dynamic-slice.2
  365.2 12.1 %all-reduce = bf16[1024]{0:T(1024)(128)(2,1)S(1)} all-reduce(bf16[1024]{0:T(1024)(128)(2,1)S(1)} %get-tuple-element.17), channel_id=3, replica_groups=mesh['tile'=8,'head'=4] {'head'}, use_global_device_ids=true, to_apply=%region_22.23.clone | all-reduce | flops 1024 | bytes 4096
  377.4 14.1 %reduce-scatter.2.cloned.1.call-done = bf16[256,512]{1,0:T(8,128)(2,1)} async-done(((bf16[1024,512]{1,0:T(8,128)(2,1)}), bf16[256,512]{1,0:T(8,128)(2,1)}) %reduce-scatter.2.cloned.1.call-update) | async-done | bytes 262160 | tf_op jit(solution)/shard_map/reduce_scatter | solution.py:147
  391.5 2.0 fusion.11
  (106 shorter events, 6.4 us)
Async XLA Ops:
  6.5 292.3 %copy-start = (bf16[512,512]{1,0:T(8,128)(2,1)S(1)}, bf16[512,512]{1,0:T(8,128)(2,1)}, u32[]{:S(2)}) copy-start(bf16[512,512]{1,0:T(8,128)(2,1)} %param.31) | copy-start | bytes 1572868
  6.5 326.0 %all-gather.3.cloned.1.call-start = ((), (), s32[]{:S(2)}) async-start(), calls=%async_computation.1 | async-start | bytes 2359296 | tf_op jit(solution)/shard_map/all_gather | solution.py:116
  92.7 3.8 collective-permute-start
  94.0 5.7 %collective-permute-start.1 = (bf16[1,128,512]{2,1,0:T(8,128)(2,1)S(1)}, bf16[1,128,512]{2,1,0:T(8,128)(2,1)S(1)}, u32[]{:S(2)}, u32[]{:S(2)}) collective-permute-start(bf16[1,128,512]{2,1,0:T(8,128)(2,1)S(1)} %get-tuple-element.37), channel_id=1, source_target_pairs={{4,0},{8,4},{12,8},{16,12},{20,16},{24,20},{28,24},{5,1},{9,5},{13... | collective-permute-start | bytes 393224 | tf_op jit(solution)/shard_map/ppermute | solution.py:36
  99.8 9.0 %copy-start.7 = (bf16[3,3,512,512]{3,2,1,0:T(8,128)(2,1)S(1)}, bf16[3,3,512,512]{3,2,1,0:T(8,128)(2,1)}, u32[]{:S(2)}) copy-start(bf16[3,3,512,512]{3,2,1,0:T(8,128)(2,1)} %param.21) | copy-start | bytes 14155780
  99.8 4.0 %collective-permute-start.2 = (bf16[4,1,512]{2,1,0:T(2,128)(2,1)S(1)}, bf16[4,1,512]{2,1,0:T(2,128)(2,1)S(1)}, u32[]{:S(2)}, u32[]{:S(2)}) collective-permute-start(bf16[4,1,512]{2,1,0:T(2,128)(2,1)S(1)} %get-tuple-element.32), channel_id=1, source_target_pairs={{0,1},{1,2},{2,3},{4,5},{5,6},{6,7},{8,9},{9,10},{10,11},{12,13},{... | collective-permute-start | bytes 12296 | tf_op jit(solution)/shard_map/ppermute | solution.py:35
  102.4 6.4 %copy-start.2 = (f32[512]{0:T(512)S(1)}, f32[512]{0:T(512)}, u32[]{:S(2)}) copy-start(f32[512]{0:T(512)} %param.22) | copy-start | bytes 6148
  102.4 6.4 %copy-start.6 = (pred[8,17]{0,1:T(8,128)(4,1)S(1)}, pred[8,17]{0,1:T(8,128)(4,1)}, u32[]{:S(2)}) copy-start(pred[8,17]{0,1:T(8,128)(4,1)} %constant.77) | copy-start | bytes 412
  102.5 5.5 %collective-permute-start.3 = (bf16[4,1,512]{2,1,0:T(2,128)(2,1)S(1)}, bf16[4,1,512]{2,1,0:T(2,128)(2,1)S(1)}, u32[]{:S(2)}, u32[]{:S(2)}) collective-permute-start(bf16[4,1,512]{2,1,0:T(2,128)(2,1)S(1)} %get-tuple-element.33), channel_id=1, source_target_pairs={{1,0},{2,1},{3,2},{5,4},{6,5},{7,6},{9,8},{10,9},{11,10},{13,12},{... | collective-permute-start | bytes 12296 | tf_op jit(solution)/shard_map/ppermute | solution.py:36
  110.3 83.4 %copy-start.3 = (f32[512]{0:T(512)S(1)}, f32[512]{0:T(512)}, u32[]{:S(2)}) copy-start(f32[512]{0:T(512)} %param.24) | copy-start | bytes 6148
  110.3 83.4 %copy-start.4 = (f32[512]{0:T(512)S(1)}, f32[512]{0:T(512)}, u32[]{:S(2)}) copy-start(f32[512]{0:T(512)} %param.23) | copy-start | bytes 6148
  194.0 2.8 collective-permute-start.4
  195.3 5.7 %collective-permute-start.5 = (bf16[1,128,512]{2,1,0:T(8,128)(2,1)S(1)}, bf16[1,128,512]{2,1,0:T(8,128)(2,1)S(1)}, u32[]{:S(2)}, u32[]{:S(2)}) collective-permute-start(bf16[1,128,512]{2,1,0:T(8,128)(2,1)S(1)} %get-tuple-element.35), channel_id=1, source_target_pairs={{4,0},{8,4},{12,8},{16,12},{20,16},{24,20},{28,24},{5,1},{9,5},{13... | collective-permute-start | bytes 393224 | tf_op jit(solution)/shard_map/ppermute | solution.py:36
  201.1 4.8 %collective-permute-start.6 = (bf16[4,1,512]{2,1,0:T(2,128)(2,1)S(1)}, bf16[4,1,512]{2,1,0:T(2,128)(2,1)S(1)}, u32[]{:S(2)}, u32[]{:S(2)}) collective-permute-start(bf16[4,1,512]{2,1,0:T(2,128)(2,1)S(1)} %get-tuple-element.28), channel_id=1, source_target_pairs={{0,1},{1,2},{2,3},{4,5},{5,6},{6,7},{8,9},{9,10},{10,11},{12,13},{... | collective-permute-start | bytes 12296 | tf_op jit(solution)/shard_map/ppermute | solution.py:35
  204.5 5.5 %collective-permute-start.7 = (bf16[4,1,512]{2,1,0:T(2,128)(2,1)S(1)}, bf16[4,1,512]{2,1,0:T(2,128)(2,1)S(1)}, u32[]{:S(2)}, u32[]{:S(2)}) collective-permute-start(bf16[4,1,512]{2,1,0:T(2,128)(2,1)S(1)} %get-tuple-element.30), channel_id=1, source_target_pairs={{1,0},{2,1},{3,2},{5,4},{6,5},{7,6},{9,8},{10,9},{11,10},{13,12},{... | collective-permute-start | bytes 12296 | tf_op jit(solution)/shard_map/ppermute | solution.py:36
  214.6 1.0 copy-start.1
  214.6 0.9 copy-start.5
  215.1 83.7 %copy-start.12 = (f32[512]{0:T(512)S(1)}, f32[512]{0:T(512)}, u32[]{:S(2)}) copy-start(f32[512]{0:T(512)} %param.28) | copy-start | bytes 6148
  215.1 83.7 %copy-start.13 = (f32[512]{0:T(512)S(1)}, f32[512]{0:T(512)}, u32[]{:S(2)}) copy-start(f32[512]{0:T(512)} %param.27) | copy-start | bytes 6148
  215.7 84.2 %copy-start.8 = (bf16[512,512]{1,0:T(8,128)(2,1)S(1)}, bf16[512,512]{1,0:T(8,128)(2,1)}, u32[]{:S(2)}) copy-start(bf16[512,512]{1,0:T(8,128)(2,1)} %param.32) | copy-start | bytes 1572868
  215.7 84.2 %copy-start.11 = (f32[512]{0:T(512)S(1)}, f32[512]{0:T(512)}, u32[]{:S(2)}) copy-start(f32[512]{0:T(512)} %param.33) | copy-start | bytes 6148
  298.7 2.3 copy-start.9
  298.7 2.3 copy-start.14
  299.9 56.7 %all-gather.5.cloned.1.call-start = ((), (), s32[]{:S(2)}) async-start(), calls=%async_computation.2 | async-start | bytes 2359296 | tf_op jit(solution)/shard_map/all_gather | solution.py:140
  301.0 90.5 %reduce-scatter.2.cloned.1.call-start = ((), (), s32[]{:S(2)}) async-start(), calls=%async_computation.3 | async-start | bytes 1310720 | tf_op jit(solution)/shard_map/reduce_scatter | solution.py:147
  301.4 9.1 %collective-permute-start.8 = (bf16[256,512]{1,0:T(8,128)(2,1)S(1)}, bf16[256,512]{1,0:T(8,128)(2,1)S(1)}, u32[]{:S(2)}, u32[]{:S(2)}) collective-permute-start(bf16[256,512]{1,0:T(8,128)(2,1)S(1)} %fusion.12), channel_id=1, source_target_pairs={{0,1},{1,2},{2,3},{3,0},{4,5},{5,6},{6,7},{7,4},{8,9},{9,10},{10,1... | collective-permute-start | bytes 786440 | tf_op jit(solution)/shard_map/ppermute | solution.py:15
  310.4 8.2 %collective-permute-start.9 = (bf16[256,512]{1,0:T(8,128)(2,1)S(1)}, bf16[256,512]{1,0:T(8,128)(2,1)S(1)}, u32[]{:S(2)}, u32[]{:S(2)}) collective-permute-start(bf16[256,512]{1,0:T(8,128)(2,1)S(1)} %collective-permute-done.8), channel_id=1, source_target_pairs={{0,1},{1,2},{2,3},{3,0},{4,5},{5,6},{6,7},{7,4},{8,9},{9,10},{10,1... | collective-permute-start | bytes 786440 | tf_op jit(solution)/shard_map/ppermute | solution.py:15
  318.6 8.2 %collective-permute-start.10 = (bf16[256,512]{1,0:T(8,128)(2,1)S(1)}, bf16[256,512]{1,0:T(8,128)(2,1)S(1)}, u32[]{:S(2)}, u32[]{:S(2)}) collective-permute-start(bf16[256,512]{1,0:T(8,128)(2,1)S(1)} %collective-permute-done.9), channel_id=1, source_target_pairs={{0,1},{1,2},{2,3},{3,0},{4,5},{5,6},{6,7},{7,4},{8,9},{9,10},{10,1... | collective-permute-start | bytes 786440 | tf_op jit(solution)/shard_map/ppermute | solution.py:15
  356.5 7.4 %copy-start.16 = (u32[32]{0:T(128)S(1)}, u32[32]{0:T(128)}, u32[]{:S(2)}) copy-start(u32[32]{0:T(128)} %constant.83) | copy-start | bytes 388
  356.5 35.0 %copy-start.10 = (bf16[512,512]{1,0:T(8,128)(2,1)S(1)}, bf16[512,512]{1,0:T(8,128)(2,1)}, u32[]{:S(2)}) copy-start(bf16[512,512]{1,0:T(8,128)(2,1)} %param.34) | copy-start | bytes 1572868
  356.5 35.0 %copy-start.15 = (f32[512]{0:T(512)S(1)}, f32[512]{0:T(512)}, u32[]{:S(2)}) copy-start(f32[512]{0:T(512)} %param.35) | copy-start | bytes 6148
Sparse Core Ops, SparseCore 0:
  300.0 26.7 all-gather.2
  328.7 27.7 all-gather.4
  364.1 27.3 reduce-scatter.1
